TPU v7x, 256 devices: a whole 4x4x8 slice. The times are simulated.
256 devices in a mesh: region: 64 (over y, z, core), strip: 4 (over x).
Axes of the slice: x: 4, y: 4, z: 8, core: 2. Of those that a mesh axis runs over, the one named last changes fastest.
Arguments:
- features: bfloat16 [32, 512, 32, 128], P(None, 'region', 'strip'), may hold values from -28 to 28
- brick_mask: int32 [64, 4, 16], P('region', 'strip'), may hold values from 0 to 1, as said below
- conv_first: bfloat16 [3, 3, 3, 32, 32], replicated, may hold values from -0.21875 to 0.21875
- conv_second: bfloat16 [3, 3, 3, 32, 32], replicated, may hold values from -0.21875 to 0.21875
- gain_first: float32 [32], replicated, may hold values from 0.5 to 1.5
- shift_first: float32 [32], replicated, may hold values from -2 to 2
- gain_second: float32 [32], replicated, may hold values from 0.5 to 1.5
- shift_second: float32 [32], replicated, may hold values from -2 to 2
Outputs:
- block_out: bfloat16 [32, 512, 32, 128], P(None, 'region', 'strip')
Inputs may be any that keep to these rules, and one draw needn't show every extreme that they name: `brick_mask`: every device's block of 1 x 1 x 16 bricks holds at least one active brick.
All inputs are finite; a program needn't handle non-finite values.
Results may differ from a plain program's by a relative error of at most 0.0085.
Values may be sent and summed in bfloat16 or wider, within the bound.
A program may use at most 64 MiB of HBM per device.

v0:
```python
import jax
import jax.numpy as jnp
from jax import lax
from jax.sharding import Mesh
from jax.sharding import PartitionSpec as P

BRICK = 8
REGION = ("region_0", "region_1", "region_2")


EPSILON = 1e-05


def from_everyone(array, axis):
    size = lax.axis_size(axis)
    return lax.all_to_all(
        jnp.broadcast_to(array[None], (size, *array.shape)), axis, 0, 0, tiled=True
    )


def taken_together(array, axis):
    everything = from_everyone(array, axis)
    return jnp.sum(everything, axis=0)


def one_axis_at_a_time(array, axes):
    far, near = axes
    return taken_together(taken_together(array, near), far)


def in_one(arrays, axis):
    ends = [0]
    for a in arrays:
        ends.append(ends[-1] + a.size)
    so_far = one_axis_at_a_time(jnp.concatenate([a.ravel() for a in arrays]), axis)
    return tuple((so_far[b:e].reshape(a.shape) for a, b, e in zip(arrays, ends, ends[1:])))


def with_halo(block, sides, width):
    for axis, dim in sides:
        count = lax.axis_size(axis)
        forward = [(i, i + 1) for i in range(count - 1)]
        backward = [(target, source) for source, target in forward]
        low = lax.ppermute(
            lax.slice_in_dim(block, block.shape[dim] - width, None, axis=dim), axis, forward
        )
        high = lax.ppermute(lax.slice_in_dim(block, 0, width, axis=dim), axis, backward)
        block = jnp.concatenate([low, block, high], axis=dim)
    return block


def expand(bricks):
    count_x, count_y, count_z = bricks.shape
    values = bricks.astype(jnp.float32)
    grown = jnp.broadcast_to(
        values[:, None, :, None, :, None], (count_x, BRICK, count_y, BRICK, count_z, BRICK)
    )
    return grown.reshape(count_x * BRICK, count_y * BRICK, count_z * BRICK)


def convolve(padded, weight, extent_x, extent_y):
    depth = padded.shape[3]
    channels = padded.shape[0]
    framed = jnp.pad(padded, ((0, 0), (0, 0), (0, 0), (1, 1)))
    flat_kernel = weight.reshape(27 * channels, weight.shape[4])
    pieces = []
    for start in range(0, extent_x, 2):
        width = min(2, extent_x - start)
        windows = []
        for step_x in range(3):
            for step_y in range(3):
                for step_z in range(3):
                    windows.append(
                        framed[
                            :,
                            start + step_x : start + step_x + width,
                            step_y : step_y + extent_y,
                            step_z : step_z + depth,
                        ]
                    )
        stacked = jnp.concatenate(windows, axis=0)
        pieces.append(
            jnp.einsum("ko,kxyz->oxyz", flat_kernel, stacked, preferred_element_type=jnp.float32)
        )
    return jnp.concatenate(pieces, axis=1)


def moments(values, voxel_mask):
    active_total, channel_sums, channel_squares = in_one(
        (
            jnp.sum(voxel_mask),
            jnp.sum(values * voxel_mask, axis=(1, 2, 3)),
            jnp.sum(values * values * voxel_mask, axis=(1, 2, 3)),
        ),
        (("region_0", "region_1"), ("region_2", "strip")),
    )
    average = channel_sums / active_total
    variance = channel_squares / active_total - average * average
    return (average, variance)


def normalize(values, average, variance, gain, shift):
    scale = lax.rsqrt(variance + EPSILON) * gain
    return (values - average[:, None, None, None]) * scale[:, None, None, None] + shift[
        :, None, None, None
    ]


def per_device(
    features,
    brick_mask,
    conv_first,
    conv_second,
    gain_first,
    shift_first,
    gain_second,
    shift_second,
):
    voxel_mask = expand(brick_mask)
    masked_input = features * voxel_mask.astype(jnp.bfloat16)
    channels, extent_x, extent_y, depth = features.shape
    stacked = jnp.concatenate([masked_input, voxel_mask.astype(jnp.bfloat16)[None]], axis=0)
    deep_block = with_halo(stacked, ((REGION, 1), ("strip", 2)), 2)
    cycle_mask = deep_block[channels, 1:-1, 1:-1].astype(jnp.float32)
    wide_out = (
        convolve(deep_block[:channels], conv_first, extent_x + 2, extent_y + 2) * cycle_mask
    ).astype(jnp.bfloat16)
    first_out = wide_out[:, 1:-1, 1:-1]
    average, variance = moments(first_out.astype(jnp.float32), voxel_mask)
    widened = normalize(wide_out.astype(jnp.float32), average, variance, gain_first, shift_first)
    second_in = (jax.nn.relu(widened) * cycle_mask).astype(jnp.bfloat16)
    second_out = (convolve(second_in, conv_second, extent_x, extent_y) * voxel_mask).astype(
        jnp.bfloat16
    )
    second_values = second_out.astype(jnp.float32)
    average, variance = moments(second_values, voxel_mask)
    result = (
        jax.nn.relu(
            normalize(second_values, average, variance, gain_second, shift_second)
            + masked_input.astype(jnp.float32)
        )
        * voxel_mask
    )
    return result.astype(jnp.bfloat16)


def solution(mesh):
    split = Mesh(
        mesh.devices.reshape(4, 8, 2, mesh.shape["strip"]),
        ("region_0", "region_1", "region_2", "strip"),
    )
    in_specs = (
        P(None, REGION, "strip", None),
        P(REGION, "strip", None),
        P(),
        P(),
        P(),
        P(),
        P(),
        P(),
    )
    out_specs = P(None, REGION, "strip", None)
    return jax.shard_map(
        per_device, mesh=split, in_specs=in_specs, out_specs=out_specs, check_vma=False
    )
```

profile of v0, /device:TPU:1, one launch (start us, length us, event | category | flops | bytes accessed | tf_op | source)
XLA Modules:
  0.0 108.8 jit_solution(7425179245910582319)
XLA Ops:
  0.0 0.7 convert_bitcast_fusion
  0.9 1.3 %copy_multiply_fusion = bf16[32,8,8,128]{3,0,2,1:T(8,128)(2,1)S(1)} fusion(bf16[32,8,8,128]{3,2,1,0:T(8,128)(2,1)} %param.8, bf16[128]{0:T(256)(128)(2,1)S(1)} %convert_element_type.40), kind=kLoop, calls=%fused_computation.158 | loop fusion | flops 262144 | bytes 1048832 | tf_op jit(solution)/shard_map/mul | solution.py:120
  2.3 4.9 %collective-permute-start = (bf16[33,2,8,128]{3,0,2,1:T(8,128)(2,1)S(1)}, bf16[33,2,8,128]{3,0,2,1:T(8,128)(2,1)S(1)}, u32[]{:S(2)}, u32[]{:S(2)}) collective-permute-start(bf16[33,2,8,128]{3,0,2,1:T(8,128)(2,1)S(1)} %get-tuple-element.174), channel_id=1, source_target_pairs={{0,4},{4,8},{8,12},{12,16},{16,20},{20,24},{24,28},{28,32},{32,36}... | collective-permute-start | bytes 405512 | tf_op jit(solution)/shard_map/ppermute | solution.py:44
  7.2 1.9 %collective-permute-start.1 = (bf16[33,2,8,128]{3,0,2,1:T(8,128)(2,1)S(1)}, bf16[33,2,8,128]{3,0,2,1:T(8,128)(2,1)S(1)}, u32[]{:S(2)}, u32[]{:S(2)}) collective-permute-start(bf16[33,2,8,128]{3,0,2,1:T(8,128)(2,1)S(1)} %get-tuple-element.175), channel_id=1, source_target_pairs={{4,0},{8,4},{12,8},{16,12},{20,16},{24,20},{28,24},{32,28},{36,32}... | collective-permute-start | bytes 405512 | tf_op jit(solution)/shard_map/ppermute | solution.py:47
  9.1 0.3 collective-permute-done
  9.5 4.4 %collective-permute-done.1 = bf16[33,2,8,128]{3,0,2,1:T(8,128)(2,1)S(1)} collective-permute-done((bf16[33,2,8,128]{3,0,2,1:T(8,128)(2,1)S(1)}, bf16[33,2,8,128]{3,0,2,1:T(8,128)(2,1)S(1)}, u32[]{:S(2)}, u32[]{:S(2)}) %collective-permute-start.1) | collective-permute-done | bytes 135200 | tf_op jit(solution)/shard_map/ppermute | solution.py:47
  13.9 3.1 %collective-permute-start.2 = (bf16[33,12,2,128]{3,0,2,1:T(8,128)(2,1)S(1)}, bf16[33,12,2,128]{3,0,2,1:T(8,128)(2,1)S(1)}, u32[]{:S(2)}, u32[]{:S(2)}) collective-permute-start(bf16[33,12,2,128]{3,0,2,1:T(8,128)(2,1)S(1)} %get-tuple-element.132), channel_id=1, source_target_pairs={{0,1},{1,2},{2,3},{4,5},{5,6},{6,7},{8,9},{9,10},{10,11},{12,13},{... | collective-permute-start | bytes 608264 | tf_op jit(solution)/shard_map/ppermute | solution.py:44
  17.0 1.3 %collective-permute-start.3 = (bf16[33,12,2,128]{3,0,2,1:T(8,128)(2,1)S(1)}, bf16[33,12,2,128]{3,0,2,1:T(8,128)(2,1)S(1)}, u32[]{:S(2)}, u32[]{:S(2)}) collective-permute-start(bf16[33,12,2,128]{3,0,2,1:T(8,128)(2,1)S(1)} %get-tuple-element.133), channel_id=1, source_target_pairs={{1,0},{2,1},{3,2},{5,4},{6,5},{7,6},{9,8},{10,9},{11,10},{13,12},{... | collective-permute-start | bytes 608264 | tf_op jit(solution)/shard_map/ppermute | solution.py:47
  18.3 0.6 broadcast_reduce_fusion
  19.0 1.2 %collective-permute-done.2 = bf16[33,12,2,128]{3,0,2,1:T(8,128)(2,1)S(1)} collective-permute-done((bf16[33,12,2,128]{3,0,2,1:T(8,128)(2,1)S(1)}, bf16[33,12,2,128]{3,0,2,1:T(8,128)(2,1)S(1)}, u32[]{:S(2)}, u32[]{:S(2)}) %collective-permute-start.2) | collective-permute-done | bytes 202784 | tf_op jit(solution)/shard_map/ppermute | solution.py:44
  20.2 3.9 %collective-permute-done.3 = bf16[33,12,2,128]{3,0,2,1:T(8,128)(2,1)S(1)} collective-permute-done((bf16[33,12,2,128]{3,0,2,1:T(8,128)(2,1)S(1)}, bf16[33,12,2,128]{3,0,2,1:T(8,128)(2,1)S(1)}, u32[]{:S(2)}, u32[]{:S(2)}) %collective-permute-start.3) | collective-permute-done | bytes 202784 | tf_op jit(solution)/shard_map/ppermute | solution.py:47
  24.1 0.3 pad_maximum_fusion
  24.4 0.3 slice.950
  24.8 1.6 %pad_maximum_fusion.1 = (bf16[33,12,10,128]{3,0,2,1:T(8,128)(2,1)S(1)}, bf16[33,12,10,128]{3,0,2,1:T(8,128)(2,1)S(1)}) fusion(bf16[33,12,2,128]{3,0,2,1:T(8,128)(2,1)S(1)} %collective-permute-done.3, bf16[33,2,8,128]{3,0,2,1:T(8,128)(2,1)S(1)} %collective-permute-done.1, bf16[1,8,8,128]{3,0,2,1:T(2,128)(2,1)S(1)} %broadcast_in_dim.21, ...), kind=kLoop, calls=%fused_computation.129 | loop fusion | flops 10137600 | bytes 3244032 | tf_op jit(solution)/shard_map/concatenate | solution.py:48
  29.3 0.4 constant_dynamic-update-slice_fusion.116
  30.0 0.4 constant_dynamic-update-slice_fusion.114
  30.3 0.4 constant_dynamic-update-slice_fusion.113
  31.0 0.4 constant_dynamic-update-slice_fusion.111
  31.4 0.4 constant_dynamic-update-slice_fusion.110
  32.1 0.4 constant_dynamic-update-slice_fusion.108
  33.0 0.3 constant_dynamic-update-slice_fusion.95
  33.7 0.3 constant_dynamic-update-slice_fusion.92
  35.1 0.3 constant_dynamic-update-slice_fusion.86
  35.8 0.9 fusion.4
  36.7 0.3 constant_dynamic-update-slice_fusion.83
  37.5 0.9 fusion.3
  38.4 0.9 fusion.2
  39.3 0.9 fusion.1
  40.2 0.9 fusion
  41.1 0.3 multiply_convert_fusion.1
  41.3 0.3 fusion.5
  41.7 0.7 pad_maximum_fusion.8
  42.4 8.5 %all_to_all.24 = f32[8,1,65]{2,1,0:T(1,128)S(1)} all-to-all(f32[8,1,65]{2,1,0:T(1,128)S(1)} %broadcast_in_dim.23), channel_id=1, replica_groups=mesh['region_0'=4,'region_1'=8,'region_2'=2,'strip'=4] {'region_2','strip'}, dimensions={0} | all-to-all | bytes 4160 | tf_op jit(solution)/shard_map/all_to_all | solution.py:16
  50.9 21.9 %all_to_all.25 = f32[32,1,65]{2,1,0:T(1,128)S(1)} all-to-all(f32[32,1,65]{2,1,0:T(1,128)S(1)} %broadcast_in_dim.24), channel_id=1, replica_groups=mesh['region_0'=4,'region_1'=8,'region_2'=2,'strip'=4] {'region_0','regi..., dimensions={0} | all-to-all | bytes 16640 | tf_op jit(solution)/shard_map/all_to_all | solution.py:16
  73.0 0.5 multiply_convert_fusion
  76.0 0.3 constant_dynamic-update-slice_fusion.138
  76.4 0.3 constant_dynamic-update-slice_fusion.137
  77.0 0.3 constant_dynamic-update-slice_fusion.135
  79.0 0.7 convolution_bitcast_fusion.8
  80.0 0.7 convolution_bitcast_fusion.7
  82.4 0.7 convolution_bitcast_fusion.6
  84.6 0.7 convolution_bitcast_fusion.5
  85.3 0.4 fusion.8
  85.7 0.7 pad_maximum_fusion.9
  86.5 9.0 %all_to_all.26 = f32[8,1,65]{2,1,0:T(1,128)S(1)} all-to-all(f32[8,1,65]{2,1,0:T(1,128)S(1)} %broadcast_in_dim.25), channel_id=1, replica_groups=mesh['region_0'=4,'region_1'=8,'region_2'=2,'strip'=4] {'region_2','strip'}, dimensions={0} | all-to-all | bytes 4160 | tf_op jit(solution)/shard_map/all_to_all | solution.py:16
  95.5 11.6 %all_to_all.27 = f32[32,1,65]{2,1,0:T(1,128)S(1)} all-to-all(f32[32,1,65]{2,1,0:T(1,128)S(1)} %broadcast_in_dim.26), channel_id=1, replica_groups=mesh['region_0'=4,'region_1'=8,'region_2'=2,'strip'=4] {'region_0','regi..., dimensions={0} | all-to-all | bytes 16640 | tf_op jit(solution)/shard_map/all_to_all | solution.py:16
  107.3 0.5 fusion.16
  107.8 1.0 copy.56
  (157 shorter events, 14.7 us)
Async XLA Ops:
  0.0 35.8 %copy-start = (bf16[3,3,3,32,32]{4,3,2,1,0:T(8,128)(2,1)S(1)}, bf16[3,3,3,32,32]{4,3,2,1,0:T(8,128)(2,1)}, u32[]{:S(2)}) copy-start(bf16[3,3,3,32,32]{4,3,2,1,0:T(8,128)(2,1)} %param.10) | copy-start | bytes 165892
  2.3 7.2 %collective-permute-start = (bf16[33,2,8,128]{3,0,2,1:T(8,128)(2,1)S(1)}, bf16[33,2,8,128]{3,0,2,1:T(8,128)(2,1)S(1)}, u32[]{:S(2)}, u32[]{:S(2)}) collective-permute-start(bf16[33,2,8,128]{3,0,2,1:T(8,128)(2,1)S(1)} %get-tuple-element.174), channel_id=1, source_target_pairs={{0,4},{4,8},{8,12},{12,16},{16,20},{20,24},{24,28},{28,32},{32,36}... | collective-permute-start | bytes 405512 | tf_op jit(solution)/shard_map/ppermute | solution.py:44
  7.2 6.6 %collective-permute-start.1 = (bf16[33,2,8,128]{3,0,2,1:T(8,128)(2,1)S(1)}, bf16[33,2,8,128]{3,0,2,1:T(8,128)(2,1)S(1)}, u32[]{:S(2)}, u32[]{:S(2)}) collective-permute-start(bf16[33,2,8,128]{3,0,2,1:T(8,128)(2,1)S(1)} %get-tuple-element.175), channel_id=1, source_target_pairs={{4,0},{8,4},{12,8},{16,12},{20,16},{24,20},{28,24},{32,28},{36,32}... | collective-permute-start | bytes 405512 | tf_op jit(solution)/shard_map/ppermute | solution.py:47
  13.9 6.2 %collective-permute-start.2 = (bf16[33,12,2,128]{3,0,2,1:T(8,128)(2,1)S(1)}, bf16[33,12,2,128]{3,0,2,1:T(8,128)(2,1)S(1)}, u32[]{:S(2)}, u32[]{:S(2)}) collective-permute-start(bf16[33,12,2,128]{3,0,2,1:T(8,128)(2,1)S(1)} %get-tuple-element.132), channel_id=1, source_target_pairs={{0,1},{1,2},{2,3},{4,5},{5,6},{6,7},{8,9},{9,10},{10,11},{12,13},{... | collective-permute-start | bytes 608264 | tf_op jit(solution)/shard_map/ppermute | solution.py:44
  17.0 7.0 %collective-permute-start.3 = (bf16[33,12,2,128]{3,0,2,1:T(8,128)(2,1)S(1)}, bf16[33,12,2,128]{3,0,2,1:T(8,128)(2,1)S(1)}, u32[]{:S(2)}, u32[]{:S(2)}) collective-permute-start(bf16[33,12,2,128]{3,0,2,1:T(8,128)(2,1)S(1)} %get-tuple-element.133), channel_id=1, source_target_pairs={{1,0},{2,1},{3,2},{5,4},{6,5},{7,6},{9,8},{10,9},{11,10},{13,12},{... | collective-permute-start | bytes 608264 | tf_op jit(solution)/shard_map/ppermute | solution.py:47
  40.1 32.7 %copy-start.5 = (f32[32]{0:T(128)S(1)}, f32[32]{0:T(128)}, u32[]{:S(2)}) copy-start(f32[32]{0:T(128)} %param.12) | copy-start | bytes 388
  40.2 32.9 %copy-start.3 = (f32[32]{0:T(128)S(1)}, f32[32]{0:T(128)}, u32[]{:S(2)}) copy-start(f32[32]{0:T(128)} %param.13) | copy-start | bytes 388
  78.1 0.9 copy-start.1
  84.4 22.8 %copy-start.6 = (f32[32]{0:T(128)S(1)}, f32[32]{0:T(128)}, u32[]{:S(2)}) copy-start(f32[32]{0:T(128)} %param.14) | copy-start | bytes 388
  84.4 22.9 %copy-start.2 = (bf16[32,8,8,128]{3,2,1,0:T(8,128)(2,1)S(1)}, bf16[32,8,8,128]{3,2,1,0:T(8,128)(2,1)}, u32[]{:S(2)}) copy-start(bf16[32,8,8,128]{3,2,1,0:T(8,128)(2,1)} %param.8) | copy-start | bytes 1572868
  84.4 22.9 %copy-start.4 = (f32[32]{0:T(128)S(1)}, f32[32]{0:T(128)}, u32[]{:S(2)}) copy-start(f32[32]{0:T(128)} %param.15) | copy-start | bytes 388
where the time goes:
time: 109 us
  blocking collectives  51.1 us (47%)
  local copies, waits for them, and re-layouts  19.8 us (18%)
  starting transfers between devices  11.3 us (10%)
  waiting for transfers between devices  9.78 us (9%)
  other arithmetic  8.35 us (8%)
  matrix products  7.3 us (7%)
  between operations  1.19 us (1%)
    all_to_all x4, blocking collectives, from_everyone(): lax.all_to_all(jnp.broadcast_to(array[None], (size, *array.shape)), axis,...  51.1 us
    unnamed x147, local copies, waits for them, and re-layouts  16.8 us
    ppermute x2, waiting for transfers between devices, with_halo(): lax.ppermute(lax.slice_in_dim(block, 0, width, axis=dim), axis, backward)  8.26 us
    ppermute x2, starting transfers between devices, with_halo(): lax.ppermute(lax.slice_in_dim(block, block.shape[dim] - width, None, axis...  8.05 us
    dot_general x9, matrix products, convolve(): jnp.einsum('ko,kxyz->oxyz', flat_kernel, stacked, preferred_element_type=...  7.3 us
    ppermute x2, starting transfers between devices, with_halo(): lax.ppermute(lax.slice_in_dim(block, 0, width, axis=dim), axis, backward)  3.21 us
  transfers between devices with their start and end apart: 4, of which 4 were waited for; matrix products, arithmetic and copies ran while one was open for 1% of the time, Pallas kernels for 0%

commit v1 on v0

v1 whole, which is shorter than its diff:
```python
import functools

import jax
import jax.numpy as jnp
from jax import lax
from jax.experimental import pallas as pl
from jax.experimental.pallas import tpu as pltpu
from jax.sharding import PartitionSpec as P

MESH = pl.DeviceIdType.MESH
EPSILON = 1e-05
C = 32
NX = 8
NY = 8
NZ = 128
ROWS = C * NY
TAPS = 27
HOLE = -1e30
F32 = jnp.float32
BF16 = jnp.bfloat16
NT = (((1,), (1,)), ((), ()))
SIDES = ((1, 0), (-1, 0), (0, 1), (0, -1), (1, 1), (1, -1), (-1, 1), (-1, -1))


def three_parts(value, axis):
    high = value.astype(BF16)
    rest = value - high.astype(F32)
    middle = rest.astype(BF16)
    low = (rest - middle.astype(F32)).astype(BF16)
    return jnp.concatenate([high, middle, low], axis=axis)


def iota(shape, dim):
    return lax.broadcasted_iota(jnp.int32, shape, dim)


def one_hot(condition):
    return jnp.where(condition, 1.0, 0.0).astype(BF16)


def kernel(
    regions,
    strips,
    features,
    bricks,
    conv_first,
    conv_second,
    gain_first,
    shift_first,
    gain_second,
    shift_second,
    out,
    raw,
    bricks_v,
    weights,
    affine,
    plane_f,
    input_x,
    input_y,
    side_send,
    mid_x,
    mid_y,
    mid_send,
    act_x,
    act_y,
    second,
    spread,
    pick_main,
    pick_side,
    weights_rep,
    banded,
    final,
    gathered,
    load_sem,
    param_sem,
    store_sem,
    halo_send_sem,
    halo_recv_sem,
    sum_send_sem,
    sum_recv_sem,
):
    region = lax.axis_index("region")
    strip = lax.axis_index("strip")
    near = regions // 4
    high = lax.div(region, near)
    low = lax.rem(region, near)
    wide = 4 * strips
    cross = high * strips + strip

    loads = [
        pltpu.make_async_copy(features.at[:, x], raw.at[x], load_sem.at[x]) for x in range(NX)
    ]
    params = [
        pltpu.make_async_copy(source, target, param_sem.at[j])
        for j, (source, target) in enumerate(
            (
                (bricks, bricks_v),
                (conv_first, weights.at[0, pl.ds(0, TAPS * C)]),
                (conv_second, weights.at[1, pl.ds(0, TAPS * C)]),
                (gain_first, affine.at[0]),
                (shift_first, affine.at[1]),
                (gain_second, affine.at[2]),
                (shift_second, affine.at[3]),
            )
        )
    ]
    for copy in params[:1] + loads + params[1:]:
        copy.start()

    def there(dr, ds):
        ok = jnp.bool_(True)
        if dr > 0:
            ok = jnp.logical_and(ok, region < regions - 1)
        if dr < 0:
            ok = jnp.logical_and(ok, region > 0)
        if ds > 0:
            ok = jnp.logical_and(ok, strip < strips - 1)
        if ds < 0:
            ok = jnp.logical_and(ok, strip > 0)
        return ok

    def near_peer(k):
        return {"region": high * near + lax.rem(low + k, near), "strip": strip}

    def cross_peer(k):
        q = lax.rem(cross + k, wide)
        return {"region": lax.div(q, strips) * near + low, "strip": lax.rem(q, strips)}

    for side in (0, NX + 1):
        input_x[side] = jnp.zeros((ROWS, NZ), BF16)
        mid_x[side] = jnp.full((ROWS, NZ), HOLE, BF16)
    input_y[...] = jnp.zeros(input_y.shape, BF16)
    mid_y[...] = jnp.full(mid_y.shape, HOLE, BF16)
    act_y[...] = jnp.zeros(act_y.shape, BF16)
    weights[:, TAPS * C :, :] = jnp.zeros((2, C, C), BF16)

    barrier = pltpu.get_barrier_semaphore()
    expected = jnp.int32(near - 1 + wide - 1)
    for dr, ds in SIDES:

        @pl.when(there(dr, ds))
        def _():
            pl.semaphore_signal(
                barrier,
                inc=1,
                device_id={"region": region + dr, "strip": strip + ds},
                device_id_type=MESH,
            )

        expected = expected + there(dr, ds).astype(jnp.int32)

    @pl.loop(1, near)
    def _(k):
        pl.semaphore_signal(barrier, inc=1, device_id=near_peer(k), device_id_type=MESH)

    @pl.loop(1, wide)
    def _(k):
        pl.semaphore_signal(barrier, inc=1, device_id=cross_peer(k), device_id_type=MESH)

    def halo_copies(rnd, planes, edges, sides):
        pieces = {
            (1, 0): (planes.at[NX], planes.at[0]),
            (-1, 0): (planes.at[1], planes.at[NX + 1]),
            (0, 1): (edges.at[1], sides.at[pl.ds(1, NX), pl.ds(0, C)]),
            (0, -1): (edges.at[0], sides.at[pl.ds(1, NX), pl.ds(C, C)]),
            (1, 1): (edges.at[1, NX - 1], sides.at[0, pl.ds(0, C)]),
            (1, -1): (edges.at[0, NX - 1], sides.at[0, pl.ds(C, C)]),
            (-1, 1): (edges.at[1, 0], sides.at[NX + 1, pl.ds(0, C)]),
            (-1, -1): (edges.at[0, 0], sides.at[NX + 1, pl.ds(C, C)]),
        }
        return [
            pltpu.make_async_remote_copy(
                src_ref=pieces[dr, ds][0],
                dst_ref=pieces[dr, ds][1],
                send_sem=halo_send_sem.at[rnd, j],
                recv_sem=halo_recv_sem.at[rnd, j],
                device_id={"region": region + dr, "strip": strip + ds},
                device_id_type=MESH,
            )
            for j, (dr, ds) in enumerate(SIDES)
        ]

    first_halo = halo_copies(0, input_x, side_send, input_y)
    second_halo = halo_copies(1, mid_x, mid_send, mid_y)

    def send_halo(copies):
        for copy, (dr, ds) in zip(copies, SIDES):

            @pl.when(there(dr, ds))
            def _():
                copy.start()

    def receive_halo(copies):
        for copy, (dr, ds) in zip(copies, SIDES):

            @pl.when(there(-dr, -ds))
            def _():
                copy.wait_recv()

    params[0].wait()
    brick_rows = jnp.broadcast_to(bricks_v[...].astype(F32), (8, NZ // 8)).astype(BF16)
    brick_lanes = one_hot(iota((NZ // 8, NZ), 1) // 8 == iota((NZ // 8, NZ), 0))
    mask = jnp.dot(brick_rows, brick_lanes, preferred_element_type=F32)[0:1]
    count = jnp.sum(mask, axis=1, keepdims=True) * float(NX * NY)

    @pl.loop(0, NX)
    def _(x):
        pltpu.make_async_copy(features.at[:, x], raw.at[x], load_sem.at[x]).wait()
        plane = raw[x].astype(F32).reshape(ROWS, NZ) * mask
        input_x[x + 1] = plane.astype(BF16)
        plane_f[...] = plane
        side_send[0, x] = plane_f[pl.ds(0, C, stride=NY), :].astype(BF16)
        side_send[1, x] = plane_f[pl.ds(NY - 1, C, stride=NY), :].astype(BF16)

    pl.semaphore_wait(barrier, expected)
    send_halo(first_halo)

    spread[...] = one_hot(iota((ROWS, C), 0) // NY == iota((ROWS, C), 1))
    for j in range(4):
        pick_main[j] = one_hot(iota((NZ, ROWS), 0) == j * C + iota((NZ, ROWS), 1) // NY)
    lane = iota((TAPS * C + C, ROWS), 1)
    wanted = ((lane // 64) * 9 + 6 * ((lane // C) % 2)) * C + lane % C
    wanted = jnp.where(lane < 192, wanted, -(1 << 20))
    for dz in range(3):
        pick_side[dz] = one_hot(iota((TAPS * C + C, ROWS), 0) == wanted + dz * C)

    for copy in params[1:]:
        copy.wait()

    def build(which):
        weights_rep[...] = lax.dot_general(
            spread[...], weights[which], NT, preferred_element_type=F32
        ).astype(BF16)
        row = iota((ROWS, ROWS), 0) % NY
        step = iota((ROWS, ROWS), 1) % NY - row

        @pl.loop(0, 9)
        def _(n):
            dx = lax.div(n, 3)
            dz = lax.rem(n, 3)
            total = jnp.zeros((ROWS, ROWS), F32)
            for dy in range(3):
                tap = dx * 9 + dy * 3 + dz
                block = pl.multiple_of(lax.div(tap, 4) * NZ, NZ)
                part = jnp.dot(
                    weights_rep[:, pl.ds(block, NZ)],
                    pick_main[lax.rem(tap, 4)],
                    preferred_element_type=F32,
                )
                total = jnp.where(step == dy - 1, part, total)
            banded[
                pl.ds(pl.multiple_of(dz * ROWS, ROWS), ROWS),
                pl.ds(pl.multiple_of(dx * ROWS, ROWS), ROWS),
            ] = total.astype(BF16)

        side = (iota((ROWS, ROWS), 1) // C) % 2
        kept = jnp.logical_or(
            jnp.logical_and(side == 0, row == 0), jnp.logical_and(side == 1, row == NY - 1)
        )
        for dz in range(3):
            part = jnp.dot(weights_rep[...], pick_side[dz], preferred_element_type=F32)
            banded[dz * ROWS : (dz + 1) * ROWS, 3 * ROWS :] = jnp.where(kept, part, 0.0).astype(
                BF16
            )

    def plane_pair(planes, sides, x):
        def column(at):
            return jnp.concatenate(
                [
                    planes[pl.ds(at, 3)].reshape(3 * ROWS, NZ),
                    sides[pl.ds(at, 4)].reshape(ROWS, NZ),
                ],
                axis=0,
            )

        both = jnp.concatenate([column(x), column(x + 1)], axis=1)
        raw_out = jnp.dot(banded[...], both, preferred_element_type=F32)
        lanes = iota((ROWS, NZ), 1)
        results = []
        for p in range(2):
            below, here, above = (
                raw_out[dz * ROWS : (dz + 1) * ROWS, p * NZ : (p + 1) * NZ] for dz in range(3)
            )
            below = jnp.where(lanes == 0, 0.0, pltpu.roll(below, 1, 1))
            above = jnp.where(lanes == NZ - 1, 0.0, pltpu.roll(above, NZ - 1, 1))
            summed = (here + below + above) * mask
            results.append(summed.astype(BF16).astype(F32))
        return results

    def row_of_sums(sums, squares):
        folded = jnp.dot(
            jnp.concatenate([fold] * 3, axis=1),
            three_parts(jnp.concatenate([sums, squares], axis=1), 0),
            preferred_element_type=F32,
        )
        stacked = jnp.concatenate(
            [folded[:, :NZ], folded[:, NZ:], jnp.zeros((2 * C, NZ), F32)], axis=0
        )
        totals = lax.dot_general(
            jnp.ones((8, 3 * NZ), BF16), three_parts(stacked, 1), NT, preferred_element_type=F32
        )[0:1]
        return jnp.where(iota((1, NZ), 1) == 2 * C, count, totals)

    def sum_copy(rnd, phase, slot, k, peer):
        return pltpu.make_async_remote_copy(
            src_ref=gathered.at[rnd, phase, slot],
            dst_ref=gathered.at[rnd, phase, slot],
            send_sem=sum_send_sem.at[rnd, phase, k],
            recv_sem=sum_recv_sem.at[rnd, phase, slot],
            device_id=peer,
            device_id_type=MESH,
        )

    def phase_send(rnd, phase, size, slot, peers, value):
        gathered[rnd, phase, slot] = value

        @pl.loop(1, size)
        def _(k):
            sum_copy(rnd, phase, slot, k, peers(k)).start()

    def phase_receive(rnd, phase, size, slot, peers):
        @pl.loop(1, size)
        def _(k):
            sum_copy(rnd, phase, lax.rem(slot + k, size), k, peers(k)).wait_recv()

        total = gathered[rnd, phase, 0]
        for k in range(1, size):
            total = total + gathered[rnd, phase, k]
        return total

    def phase_finish(rnd, phase, size, slot, peers):
        @pl.loop(1, size)
        def _(k):
            sum_copy(rnd, phase, slot, k, peers(k)).wait_send()

    expand = jnp.concatenate(
        [
            one_hot(iota((ROWS, C), 0) // NY == iota((ROWS, C), 1)),
            one_hot(iota((2 * C, C), 0) % C == iota((2 * C, C), 1)),
        ],
        axis=0,
    )
    fold = one_hot(iota((C, ROWS), 1) // NY == iota((C, ROWS), 0))

    def columns(total, gain, shift):
        active = total[:, 2 * C : 2 * C + 1]
        average = total[:, :C] / active
        variance = total[:, C : 2 * C] / active - average * average
        scale = lax.rsqrt(variance + EPSILON) * gain
        offset = shift - average * scale
        rows = jnp.concatenate(
            [jnp.broadcast_to(scale, (NZ, C)), jnp.broadcast_to(offset, (NZ, C))], axis=0
        )
        both = lax.dot_general(
            jnp.concatenate([expand] * 3, axis=1),
            three_parts(rows, 1),
            NT,
            preferred_element_type=F32,
        )
        return both[:, :NZ], both[:, NZ:]

    build(0)
    receive_halo(first_halo)

    sums = jnp.zeros((ROWS, NZ), F32)
    squares = jnp.zeros((ROWS, NZ), F32)
    for x in range(0, NX, 2):
        for p, value in enumerate(plane_pair(input_x, input_y, x)):
            sums = sums + value
            squares = squares + value * value
            held = jnp.where(mask > 0.0, value, HOLE)
            mid_x[x + p + 1] = held.astype(BF16)
            plane_f[...] = held
            mid_send[0, x + p] = plane_f[pl.ds(0, C, stride=NY), :].astype(BF16)
            mid_send[1, x + p] = plane_f[pl.ds(NY - 1, C, stride=NY), :].astype(BF16)

    phase_send(0, 0, near, low, near_peer, row_of_sums(sums, squares))
    send_halo(second_halo)
    build(1)
    partial = phase_receive(0, 0, near, low, near_peer)
    phase_send(0, 1, wide, cross, cross_peer, partial)
    receive_halo(second_halo)
    total = phase_receive(0, 1, wide, cross, cross_peer)

    scale, offset = columns(total, affine[0], affine[1])
    for x in range(NX + 2):
        value = mid_x[x].astype(F32) * scale[:ROWS] + offset[:ROWS]
        act_x[x] = jnp.maximum(value, 0.0).astype(BF16)
        value = mid_y[x].astype(F32) * scale[ROWS:] + offset[ROWS:]
        act_y[x] = jnp.maximum(value, 0.0).astype(BF16)

    sums = jnp.zeros((ROWS, NZ), F32)
    squares = jnp.zeros((ROWS, NZ), F32)
    for x in range(0, NX, 2):
        for p, value in enumerate(plane_pair(act_x, act_y, x)):
            sums = sums + value
            squares = squares + value * value
            second[x + p] = value.astype(BF16)

    phase_send(1, 0, near, low, near_peer, row_of_sums(sums, squares))
    partial = phase_receive(1, 0, near, low, near_peer)
    phase_send(1, 1, wide, cross, cross_peer, partial)
    total = phase_receive(1, 1, wide, cross, cross_peer)

    scale, offset = columns(total, affine[2], affine[3])
    for x in range(NX):
        value = second[x].astype(F32) * scale[:ROWS] + offset[:ROWS]
        value = jnp.maximum(value + input_x[x + 1].astype(F32), 0.0) * mask
        final[x] = value.reshape(C, NY, NZ).astype(BF16)
        pltpu.make_async_copy(final.at[x], out.at[:, x], store_sem.at[x]).start()

    for copies in (first_halo, second_halo):
        for copy, (dr, ds) in zip(copies, SIDES):

            @pl.when(there(dr, ds))
            def _():
                copy.wait_send()

    for rnd in range(2):
        phase_finish(rnd, 0, near, low, near_peer)
        phase_finish(rnd, 1, wide, cross, cross_peer)
    for x in range(NX):
        pltpu.make_async_copy(final.at[x], out.at[:, x], store_sem.at[x]).wait()


def solution(mesh):
    regions, strips = mesh.shape["region"], mesh.shape["strip"]
    most = max(regions // 4, 4 * strips)

    def per_device(features, bricks, conv_first, conv_second, *affine):
        rows = (TAPS * C, C)
        return pl.pallas_call(
            functools.partial(kernel, regions, strips),
            out_shape=jax.ShapeDtypeStruct(features.shape, BF16),
            in_specs=[pl.BlockSpec(memory_space=pl.ANY)] * 8,
            out_specs=pl.BlockSpec(memory_space=pl.ANY),
            scratch_shapes=[
                pltpu.VMEM((NX, C, NY, NZ), BF16),
                pltpu.VMEM((1, NZ // 8), jnp.int32),
                pltpu.VMEM((2, TAPS * C + C, C), BF16),
                pltpu.VMEM((4, 1, C), F32),
                pltpu.VMEM((ROWS, NZ), F32),
                pltpu.VMEM((NX + 2, ROWS, NZ), BF16),
                pltpu.VMEM((NX + 4, 2 * C, NZ), BF16),
                pltpu.VMEM((2, NX, C, NZ), BF16),
                pltpu.VMEM((NX + 2, ROWS, NZ), BF16),
                pltpu.VMEM((NX + 2, 2 * C, NZ), BF16),
                pltpu.VMEM((2, NX, C, NZ), BF16),
                pltpu.VMEM((NX + 2, ROWS, NZ), BF16),
                pltpu.VMEM((NX + 4, 2 * C, NZ), BF16),
                pltpu.VMEM((NX, ROWS, NZ), BF16),
                pltpu.VMEM((ROWS, C), BF16),
                pltpu.VMEM((4, NZ, ROWS), BF16),
                pltpu.VMEM((3, TAPS * C + C, ROWS), BF16),
                pltpu.VMEM((ROWS, TAPS * C + C), BF16),
                pltpu.VMEM((3 * ROWS, 4 * ROWS), BF16),
                pltpu.VMEM((NX, C, NY, NZ), BF16),
                pltpu.VMEM((2, 2, most, 1, NZ), F32),
                pltpu.SemaphoreType.DMA((NX,)),
                pltpu.SemaphoreType.DMA((7,)),
                pltpu.SemaphoreType.DMA((NX,)),
                pltpu.SemaphoreType.DMA((2, 8)),
                pltpu.SemaphoreType.DMA((2, 8)),
                pltpu.SemaphoreType.DMA((2, 2, most)),
                pltpu.SemaphoreType.DMA((2, 2, most)),
            ],
            compiler_params=pltpu.CompilerParams(
                collective_id=0, has_side_effects=True, vmem_limit_bytes=48 * 1024 * 1024
            ),
            name="block",
        )(
            features,
            bricks.reshape(1, NZ // 8),
            conv_first.reshape(rows),
            conv_second.reshape(rows),
            *(a.reshape(1, C) for a in affine),
        )

    placed = P(None, "region", "strip", None)
    return jax.shard_map(
        per_device,
        mesh=mesh,
        in_specs=(placed, P("region", "strip", None)) + (P(),) * 6,
        out_specs=placed,
        check_vma=False,
    )
```

time: 109 us -> 46.7 us (0.43)
  blocking collectives: 51.1 us -> 0 us
  Pallas kernels: 0 us -> 42.1 us
  local copies, waits for them, and re-layouts: 19.8 us -> 4.4 us
  starting transfers between devices: 11.3 us -> 0 us
  waiting for transfers between devices: 9.78 us -> 0 us
  other arithmetic: 8.35 us -> 0 us
  matrix products: 7.3 us -> 0 us
  between operations: 1.19 us -> 0.03 us
    all_to_all x4 -> x0, blocking collectives: 51.1 us -> none  [from_everyone(): lax.all_to_all(jnp.broadcast_to(array[None], (size, *array.shape)), axis,...]
    pallas_call x0 -> x1, Pallas kernels: none -> 42.1 us  [per_device(): pl.pallas_call(functools.partial(kernel, regions, strips), out_shape=jax....]
    unnamed x147 -> x17, local copies, waits for them, and re-layouts: 16.8 us -> 4.4 us
    ppermute x4 -> x0, starting transfers between devices: 11.3 us -> none  [the longest x2 8.05 us: with_halo(): lax.ppermute(lax.slice_in_dim(block, block.shape[dim] - width, None, axis...]
    ppermute x4 -> x0, waiting for transfers between devices: 9.78 us -> none  [the longest x2 8.26 us: with_halo(): lax.ppermute(lax.slice_in_dim(block, 0, width, axis=dim), axis, backward)]
    dot_general x9 -> x0, matrix products: 7.3 us -> none  [convolve(): jnp.einsum('ko,kxyz->oxyz', flat_kernel, stacked, preferred_element_type=...]
    concatenate x4 -> x0, other arithmetic: 3.31 us -> none  [the longest x2 1.86 us: with_halo(): block = jnp.concatenate([low, block, high], axis=dim)]
    mul x4 -> x0, other arithmetic: 1.61 us -> none  [the longest x1 1.34 us: per_device(): masked_input = features * voxel_mask.astype(jnp.bfloat16)]
  transfers between devices with their start and end apart: 4 -> 0, of which waited for: 4 -> 0; matrix products, arithmetic and copies ran while one was open for 1% -> 0% of each run, Pallas kernels for 0% -> 0%
where the time goes in v1:
time: 46.7 us; the launch traced here: 46.5 us
  Pallas kernels  42.1 us (90%)
  local copies, waits for them, and re-layouts  4.4 us (9%)
    pallas_call x1, Pallas kernels, per_device(): pl.pallas_call(functools.partial(kernel, regions, strips), out_shape=jax....  42.1 us
    unnamed x17, local copies, waits for them, and re-layouts  4.4 us

profile of v1, /device:TPU:1, one launch (start us, length us, event | category | flops | bytes accessed | tf_op | source)
XLA Modules:
  0.0 46.5 jit_solution(7757928889961207698)
XLA Ops:
  0.0 0.0 copy-start.6
  0.0 0.0 copy-start.7
  0.0 0.0 copy-start.3
  0.0 0.0 copy-start.4
  0.0 0.0 copy-start.5
  0.0 0.6 %copy-done.6 = f32[32]{0:T(128)S(1)} copy-done((f32[32]{0:T(128)S(1)}, f32[32]{0:T(128)}, u32[]{:S(2)}) %copy-start.6) | copy-done | bytes 152
  0.7 0.0 copy-done.7
  0.7 0.0 copy-done.3
  0.7 0.0 copy-done.4
  0.7 0.0 copy-done.5
  0.7 0.0 copy-start
  0.7 1.0 %copy-done = bf16[32,8,8,128]{3,2,1,0:T(8,128)(2,1)S(1)} copy-done((bf16[32,8,8,128]{3,2,1,0:T(8,128)(2,1)S(1)}, bf16[32,8,8,128]{3,2,1,0:T(8,128)(2,1)}, u32[]{:S(2)}) %copy-start) | copy-done | bytes 524312
  1.8 0.0 copy-start.1
  1.8 0.9 %copy-done.1 = bf16[3,3,3,32,32]{4,3,2,1,0:T(8,128)(2,1)S(1)} copy-done((bf16[3,3,3,32,32]{4,3,2,1,0:T(8,128)(2,1)S(1)}, bf16[3,3,3,32,32]{4,3,2,1,0:T(8,128)(2,1)}, u32[]{:S(2)}) %copy-start.1) | copy-done | bytes 55320
  2.7 0.0 copy-start.2
  2.7 0.9 %copy-done.2 = bf16[3,3,3,32,32]{4,3,2,1,0:T(8,128)(2,1)S(1)} copy-done((bf16[3,3,3,32,32]{4,3,2,1,0:T(8,128)(2,1)S(1)}, bf16[3,3,3,32,32]{4,3,2,1,0:T(8,128)(2,1)}, u32[]{:S(2)}) %copy-start.2) | copy-done | bytes 55320
  3.6 42.1 %block.1 = bf16[32,8,8,128]{3,2,1,0:T(8,128)(2,1)S(1)} custom-call(bf16[32,8,8,128]{3,2,1,0:T(8,128)(2,1)S(1)} %copy-done, s32[1,16]{1,0:T(1,128)S(1)} %bitcast.9, bf16[864,32]{1,0:T(8,128)(2,1)S(1)} %bitcast.7, bf16[864,32]{1,0:T(8,128)(2,1)S(1)} %bitcast.8, f32[1,32]{1,0:T(1,128)S(1)} %bitcast.10, f32[1,32]{1,0:T(1,128)S(1)} %bitcast.11, ...), custom_call_target="tpu_custom_call" | custom-call | tf_op jit(solution)/shard_map/block/pallas_call | solution.py:432
  45.7 0.8 %copy.10 = bf16[32,8,8,128]{3,2,1,0:T(8,128)(2,1)} copy(bf16[32,8,8,128]{3,2,1,0:T(8,128)(2,1)S(1)} %block.1) | data formatting | bytes 1048576
Async XLA Ops:
  0.0 0.7 %copy-start.6 = (f32[32]{0:T(128)S(1)}, f32[32]{0:T(128)}, u32[]{:S(2)}) copy-start(f32[32]{0:T(128)} %param.14) | copy-start | bytes 388
  0.0 0.7 %copy-start.7 = (f32[32]{0:T(128)S(1)}, f32[32]{0:T(128)}, u32[]{:S(2)}) copy-start(f32[32]{0:T(128)} %param.15) | copy-start | bytes 388
  0.0 0.7 %copy-start.3 = (s32[1,1,16]{2,1,0:T(1,128)S(1)}, s32[1,1,16]{2,1,0:T(1,128)}, u32[]{:S(2)}) copy-start(s32[1,1,16]{2,1,0:T(1,128)} %param.9) | copy-start | bytes 196
  0.0 0.7 %copy-start.4 = (f32[32]{0:T(128)S(1)}, f32[32]{0:T(128)}, u32[]{:S(2)}) copy-start(f32[32]{0:T(128)} %param.12) | copy-start | bytes 388
  0.0 0.7 %copy-start.5 = (f32[32]{0:T(128)S(1)}, f32[32]{0:T(128)}, u32[]{:S(2)}) copy-start(f32[32]{0:T(128)} %param.13) | copy-start | bytes 388
  0.7 1.0 %copy-start = (bf16[32,8,8,128]{3,2,1,0:T(8,128)(2,1)S(1)}, bf16[32,8,8,128]{3,2,1,0:T(8,128)(2,1)}, u32[]{:S(2)}) copy-start(bf16[32,8,8,128]{3,2,1,0:T(8,128)(2,1)} %features.1) | copy-start | bytes 1572868
  1.8 0.9 %copy-start.1 = (bf16[3,3,3,32,32]{4,3,2,1,0:T(8,128)(2,1)S(1)}, bf16[3,3,3,32,32]{4,3,2,1,0:T(8,128)(2,1)}, u32[]{:S(2)}) copy-start(bf16[3,3,3,32,32]{4,3,2,1,0:T(8,128)(2,1)} %param.10) | copy-start | bytes 165892
  2.7 0.9 %copy-start.2 = (bf16[3,3,3,32,32]{4,3,2,1,0:T(8,128)(2,1)S(1)}, bf16[3,3,3,32,32]{4,3,2,1,0:T(8,128)(2,1)}, u32[]{:S(2)}) copy-start(bf16[3,3,3,32,32]{4,3,2,1,0:T(8,128)(2,1)} %param.11) | copy-start | bytes 165892
